TPU v7x, 32 devices: a whole 2x2x4 slice. The times are simulated.
32 devices in a mesh: grp: 8 (over y, x, core), sp: 4 (over z).
Axes of the slice: x: 2, y: 2, z: 4, core: 2. Of those that a mesh axis runs over, the one named last changes fastest.
Arguments:
- latents: bfloat16 [8, 512, 3072], P('grp', 'sp'), may hold values from -6 to 6
- timestep: int32 [8], P('grp'), may hold values from 0 to 999
- w_mod: bfloat16 [256, 9216], replicated, may hold values from -0.375 to 0.375
- w_qkv: bfloat16 [4, 3072, 384], P('sp', 'grp'), may hold values from -2 to 2
- w_out: bfloat16 [4, 128, 3072], P('sp', 'grp'), may hold values from -0.5 to 0.5
Outputs:
- update: bfloat16 [8, 512, 3072], P('grp', 'sp')
All inputs are finite; a program needn't handle non-finite values.
Results may differ from a plain program's by a relative error of at most 0.012.
Values may be sent and summed in bfloat16 or wider, within the bound.
A program may use at most 128 MiB of HBM per device.

v0:
```python
import math

import jax
import jax.numpy as jnp
from jax import lax
from jax.sharding import PartitionSpec as P


def modulation(timestep, w_mod):
    half_freq = w_mod.shape[0] // 2
    freqs = jnp.exp(-math.log(10000.0) * jnp.arange(half_freq, dtype=jnp.float32) / half_freq)
    angles = timestep.astype(jnp.float32)[:, None] * freqs[None, :]
    embed = jnp.concatenate([jnp.cos(angles), jnp.sin(angles)], axis=1).astype(jnp.bfloat16)
    return jnp.dot(embed, w_mod, preferred_element_type=jnp.float32)


def normalize(latents, shift, scale):
    values = latents.astype(jnp.float32)
    center = jnp.mean(values, axis=-1, keepdims=True)
    spread = jnp.mean((values - center) ** 2, axis=-1, keepdims=True)
    normed = (values - center) * lax.rsqrt(spread + 1e-06)
    return (normed * (1.0 + scale[:, None, :]) + shift[:, None, :]).astype(jnp.bfloat16)


def attend(query, keys, values):
    length, head_size = query.shape
    block = min(512, length)
    blocks = query.reshape(length // block, block, head_size)

    def one_block(query_rows):
        scores = lax.dot_general(
            query_rows, keys, (((1,), (1,)), ((), ())), preferred_element_type=jnp.float32
        )
        scores = scores / math.sqrt(head_size)
        largest = jnp.max(scores, axis=1, keepdims=True)
        weights = jnp.exp(scores - largest)
        probs = (weights / jnp.sum(weights, axis=1, keepdims=True)).astype(jnp.bfloat16)
        return jnp.dot(probs, values, preferred_element_type=jnp.float32).astype(jnp.bfloat16)

    return lax.map(one_block, blocks).reshape(length, head_size)


def on_device(latents, timestep, w_mod, w_qkv, w_out):
    images, tok_local, width = latents.shape
    triple = w_qkv.shape[2]
    head_size = triple // 3
    mod = modulation(timestep, w_mod)
    shift = mod[:, :width]
    scale = mod[:, width : 2 * width]
    gate = mod[:, 2 * width :]
    normed = normalize(latents, shift, scale)
    whole = lax.all_gather(normed, "sp", axis=1, tiled=True)
    qkv_sum = jnp.einsum(
        "itc,cf->itf",
        whole,
        lax.all_gather(w_qkv, "grp", axis=1, tiled=True)[0],
        preferred_element_type=jnp.float32,
    )
    qkv = qkv_sum.astype(jnp.bfloat16)
    out_rows = lax.all_gather(w_out, "grp", axis=1, tiled=True)
    attended = jnp.stack(
        [
            attend(
                qkv[0, :, :head_size],
                qkv[0, :, head_size : 2 * head_size],
                qkv[0, :, 2 * head_size :],
            )
        ]
    )
    mine = lax.all_to_all(attended, "sp", split_axis=1, concat_axis=2, tiled=True)
    piece = lax.all_gather(out_rows, "sp", axis=0, tiled=True)
    count = piece.shape[0]
    mixed = mine
    mixed = mixed.reshape(images, tok_local, count, head_size)
    contrib = jnp.einsum("itnc,ncd->itnd", mixed, piece, preferred_element_type=jnp.float32).astype(
        jnp.bfloat16
    )
    contrib = lax.optimization_barrier(contrib)
    total = jnp.sum(contrib.astype(jnp.float32), axis=2)
    return (gate[:, None, :] * total).astype(jnp.bfloat16)


def solution(mesh):
    placed = (P("grp", "sp", None), P("grp"), P(), P("sp", "grp", None), P("sp", "grp", None))
    return jax.shard_map(
        on_device, mesh=mesh, in_specs=placed, out_specs=P("grp", "sp", None), check_vma=False
    )
```

profile of v0, /device:TPU:0, one launch (start us, length us, event | category | flops | bytes accessed | tf_op | source)
XLA Modules:
  0.0 184.8 jit_solution(8514768617609309561)
XLA Ops:
  6.5 0.0 all-gather.6.cloned.1.call-start
  6.5 0.7 all-gather.6.cloned.1.call-update
  7.3 0.0 all-gather.4.cloned.1.call-start
  7.9 0.1 sine_convert_fusion
  8.0 1.3 convert_reduce_fusion.1
  9.4 1.5 fusion.6
  10.9 0.0 copy-start
  10.9 3.1 %fusion.25 = f32[1,9216]{1,0:T(1,128)S(1)} fusion(bf16[256,1]{0,1:T(2,128)(2,1)S(1)} %reshape.111, bf16[256,9216]{1,0:T(8,128)(2,1)} %param.7), kind=kOutput, calls=%fused_computation.37 | convolution fusion | flops 4718592 | bytes 4755968 | tf_op jit(solution)/shard_map/dot_general | solution.py:14
  14.0 0.0 copy-start.1
  14.0 0.0 copy-done
  14.0 1.3 fusion.9
  15.3 0.0 all-gather.4.cloned.1.call-update
  15.3 0.0 all-gather.8.cloned.1.call-start
  15.4 0.0 copy-done.1
  15.4 14.1 %all_gather.14 = bf16[1,128,3072]{2,1,0:T(8,128)(2,1)} all-gather(bf16[1,16,3072]{2,1,0:T(8,128)(2,1)S(1)} %copy-done.1), channel_id=1, replica_groups=mesh['grp'=8,'sp'=4] {'grp'}, dimensions={1}, use_global_device_ids=true | all-gather | bytes 884736 | tf_op jit(solution)/shard_map/all_gather | solution.py:60
  29.5 0.0 all-gather.8.cloned.1.call-update
  29.5 12.9 %all-gather.6.cloned.1.call-done = bf16[1,3072,384]{2,1,0:T(8,128)(2,1)} async-done(((bf16[1,384,384]{2,1,0:T(8,128)(2,1)}), bf16[1,3072,384]{2,1,0:T(8,128)(2,1)}) %all-gather.6.cloned.1.call-update) | async-done | bytes 2359312 | tf_op jit(solution)/shard_map/all_gather | solution.py:56
  42.4 65.0 %all-gather.4.cloned.1.call-done = bf16[1,512,3072]{2,1,0:T(8,128)(2,1)} async-done(((bf16[1,128,3072]{2,1,0:T(8,128)(2,1)}), bf16[1,512,3072]{2,1,0:T(8,128)(2,1)}) %all-gather.4.cloned.1.call-update) | async-done | bytes 3145744 | tf_op jit(solution)/shard_map/all_gather | solution.py:52
  107.4 4.4 %fusion.16 = bf16[1,512,384]{2,1,0:T(8,128)(2,1)S(1)} fusion(bf16[1,3072,384]{2,1,0:T(8,128)(2,1)} %all-gather.6.cloned.1.call-done, bf16[1,512,3072]{2,1,0:T(8,128)(2,1)} %all-gather.4.cloned.1.call-done), kind=kOutput, calls=%fused_computation.18 | convolution fusion | flops 1208156160 | bytes 5898240 | tf_op jit(solution)/shard_map/itc,cf->itf/dot_general | solution.py:53
  111.8 0.3 fusion.24
  112.1 0.2 fusion.22
  112.3 0.4 fusion.21
  112.7 0.2 copy.10
  112.9 0.5 broadcast.81
  113.5 1.4 reduce.3
  114.9 11.8 %all_to_all.15 = bf16[4,2,8192]{2,1,0:T(2,128)(2,1)S(1)} all-to-all(bf16[4,2,8192]{2,1,0:T(2,128)(2,1)S(1)} %reshape.113), channel_id=1, replica_groups=mesh['grp'=8,'sp'=4] {'sp'}, dimensions={0} | all-to-all | bytes 262144 | tf_op jit(solution)/shard_map/all_to_all | solution.py:70
  126.7 0.1 reshape.114
  126.8 47.0 %all-gather.8.cloned.1.call-done = bf16[4,128,3072]{2,1,0:T(8,128)(2,1)} async-done(((bf16[1,128,3072]{2,1,0:T(8,128)(2,1)}), bf16[4,128,3072]{2,1,0:T(8,128)(2,1)}) %all-gather.8.cloned.1.call-update) | async-done | bytes 3145744 | tf_op jit(solution)/shard_map/all_gather | solution.py:71
  173.8 2.9 %fusion = bf16[1,128,4,3072]{3,1,2,0:T(8,128)(2,1)S(1)} fusion(bf16[128,4,128]{2,0,1:T(8,128)(2,1)S(1)} %bitcast.61, bf16[4,128,3072]{2,1,0:T(8,128)(2,1)} %all-gather.8.cloned.1.call-done), kind=kOutput, calls=%fused_computation.2 | convolution fusion | flops 404226048 | bytes 6422528 | tf_op jit(solution)/shard_map/itnc,ncd->itnd/dot_general | solution.py:75
  176.7 0.6 convert_reduce_fusion
  177.3 1.0 fusion.10
  (7 shorter events, 0.1 us)
Async XLA Ops:
  6.5 35.9 %all-gather.6.cloned.1.call-start = ((), (), s32[]{:S(2)}) async-start(), calls=%async_computation.2 | async-start | bytes 2654208 | tf_op jit(solution)/shard_map/all_gather | solution.py:56
  7.3 100.2 %all-gather.4.cloned.1.call-start = ((), (), s32[]{:S(2)}) async-start(), calls=%async_computation.1 | async-start | bytes 3932160 | tf_op jit(solution)/shard_map/all_gather | solution.py:52
  10.9 3.2 %copy-start = (bf16[1,128,3072]{2,1,0:T(8,128)(2,1)S(1)}, bf16[1,128,3072]{2,1,0:T(8,128)(2,1)}, u32[]{:S(2)}) copy-start(bf16[1,128,3072]{2,1,0:T(8,128)(2,1)} %param.5) | copy-start | bytes 2359300
  14.0 1.4 copy-start.1
  15.3 158.5 %all-gather.8.cloned.1.call-start = ((), (), s32[]{:S(2)}) async-start(), calls=%async_computation.3 | async-start | bytes 3932160 | tf_op jit(solution)/shard_map/all_gather | solution.py:71
Sparse Core Ops, SparseCore 0:
  9.2 33.1 all-gather.5
  44.0 63.4 all-gather.3
  109.0 64.7 all-gather.7
where the time goes:
time: 185 us
  waiting for transfers between devices  126 us (68%)
  blocking collectives  25.8 us (14%)
  between operations  13.9 us (8%)
  matrix products  11.1 us (6%)
  other arithmetic  7.36 us (4%)
    all_gather x1, waiting for transfers between devices, on_device(): whole = lax.all_gather(normed, 'sp', axis=1, tiled=True)  65 us
    all_gather x1, waiting for transfers between devices, on_device(): piece = lax.all_gather(out_rows, 'sp', axis=0, tiled=True)  47 us
    all_gather x1, blocking collectives, on_device(): out_rows = lax.all_gather(w_out, 'grp', axis=1, tiled=True)  14.1 us
    all_gather x1, waiting for transfers between devices, on_device(): lax.all_gather(w_qkv, 'grp', axis=1, tiled=True)[0]  12.9 us
    all_to_all x1, blocking collectives, on_device(): lax.all_to_all(attended, 'sp', split_axis=1, concat_axis=2, tiled=True)  11.8 us
    dot_general x1, matrix products, on_device(): jnp.einsum('itc,cf->itf', whole, lax.all_gather(w_qkv, 'grp', axis=1, til...  4.41 us
  transfers between devices with their start and end apart: 3, of which 3 were waited for; matrix products, arithmetic and copies ran while one was open for 8% of the time, Pallas kernels for 0%

commit v1 on v0

v1 whole, which is shorter than its diff:
```python
import functools
import math

import jax
import jax.numpy as jnp
from jax import lax
from jax.experimental import pallas as pl
from jax.experimental.pallas import tpu as pltpu
from jax.sharding import PartitionSpec as P

MESH = pl.DeviceIdType.MESH


def embedding(timestep, freq):
    half_freq = freq // 2
    freqs = jnp.exp(-math.log(10000.0) * jnp.arange(half_freq, dtype=jnp.float32) / half_freq)
    angles = timestep.astype(jnp.float32)[:, None] * freqs[None, :]
    return jnp.concatenate([jnp.cos(angles), jnp.sin(angles)], axis=1).astype(jnp.bfloat16)


def kernel(
    n_grp,
    n_sp,
    lat_hbm,
    embed_ref,
    wmod_hbm,
    wqkv_hbm,
    wout_hbm,
    out_ref,
    lat,
    wmod,
    mod,
    normed,
    wq,
    wo,
    q_buf,
    kv,
    att_mine,
    att_send,
    loc_sem,
    wz_s,
    wz_r,
    wx_s,
    wx_r,
    wd_s,
    wd_r,
    oz_s,
    oz_r,
    ox_s,
    ox_r,
    od_s,
    od_r,
    lat_s,
    lat_r,
    kv_s,
    kv_r,
    at_s,
    at_r,
):
    g = lax.axis_index("grp")
    s = lax.axis_index("sp")
    core, chip = g % 2, g // 2
    chips = n_grp // 2
    pairs = n_sp // 2
    parity, pair = s % 2, s // 2
    tok, width = lat_hbm.shape[1], lat_hbm.shape[2]
    rows_q = wqkv_hbm.shape[1]
    rows_o = wout_hbm.shape[1]
    head = wqkv_hbm.shape[2] // 3
    sib = (chip * 2 + 1 - core, s)
    mate = (g, pair * 2 + 1 - parity)

    def at_chip(c):
        return ((chip + c) % chips * 2 + core, s)

    def at_pair(k, flip):
        return (g, (pair + k) % pairs * 2 + (parity + flip) % 2)

    def remote(src, dst, ssem, rsem, device):
        return pltpu.make_async_remote_copy(
            src_ref=src, dst_ref=dst, send_sem=ssem, recv_sem=rsem, device_id=device, device_id_type=MESH
        )

    def wq_rows(k, owner):
        return wq.at[k, pl.ds(pl.multiple_of(owner * rows_q, rows_q), rows_q), :]

    def wo_rows(par, k, owner):
        first = (par * pairs + k) * head + owner * rows_o
        return wo.at[pl.ds(pl.multiple_of(first, rows_o), rows_o), :]

    barrier = pltpu.get_barrier_semaphore()
    peers = [sib] + [at_chip(c) for c in range(1, chips)]
    peers += [at_pair(k, f) for k in range(pairs) for f in range(2) if (k, f) != (0, 0)]
    for peer in peers:
        pl.semaphore_signal(barrier, inc=1, device_id=peer, device_id_type=MESH)
    local = [
        pltpu.make_async_copy(wqkv_hbm.at[0], wq_rows(0, g), loc_sem.at[0]),
        pltpu.make_async_copy(wout_hbm.at[0], wo_rows(parity, 0, g), loc_sem.at[1]),
        pltpu.make_async_copy(lat_hbm.at[0], lat.at[0], loc_sem.at[2]),
        pltpu.make_async_copy(wmod_hbm, wmod, loc_sem.at[3]),
    ]
    for copy in local:
        copy.start()
    local[0].wait()
    local[1].wait()
    local[2].wait()
    pl.semaphore_wait(barrier, len(peers))

    sends = []

    def start(*args):
        copy = remote(*args)
        copy.start()
        sends.append(copy)

    def arrive(region, ssem, rsem):
        remote(region, region, ssem, rsem, sib).wait_recv()

    for k in range(1, pairs):
        start(wq_rows(0, g), wq_rows(k, g), wz_s.at[k], wz_r.at[k], at_pair(k, 0))

    def spread_q(k):
        for c in range(1, chips):
            start(wq_rows(k, g), wq_rows(k, g), wx_s.at[k, c], wx_r.at[k, c], at_chip(c))
        start(wq_rows(k, g), wq_rows(k, g), wd_s.at[k, 0], wd_r.at[k, 0], sib)

    def pass_q(k):
        for c in range(1, chips):
            region = wq_rows(k, (chip + chips - c) % chips * 2 + core)
            arrive(region, wx_s.at[k, c], wx_r.at[k, c])
            start(region, region, wd_s.at[k, c], wd_r.at[k, c], sib)

    def finish_q(k):
        for c in range(chips):
            region = wq_rows(k, (chip + chips - c) % chips * 2 + 1 - core)
            arrive(region, wd_s.at[k, c], wd_r.at[k, c])

    def spread_o(k, flip):
        region = wo_rows((parity + flip) % 2, k, g)
        i = k * 2 + flip
        for c in range(1, chips):
            start(region, region, ox_s.at[i, c], ox_r.at[i, c], at_chip(c))
        start(region, region, od_s.at[i, 0], od_r.at[i, 0], sib)

    def pass_o(k, flip):
        i = k * 2 + flip
        for c in range(1, chips):
            region = wo_rows((parity + flip) % 2, k, (chip + chips - c) % chips * 2 + core)
            arrive(region, ox_s.at[i, c], ox_r.at[i, c])
            start(region, region, od_s.at[i, c], od_r.at[i, c], sib)

    def finish_o(k, flip):
        i = k * 2 + flip
        for c in range(chips):
            region = wo_rows((parity + flip) % 2, k, (chip + chips - c) % chips * 2 + 1 - core)
            arrive(region, od_s.at[i, c], od_r.at[i, c])

    far = [(k, f) for k in range(pairs) for f in range(2) if (k, f) != (0, 0)]

    spread_q(0)
    start(lat.at[0], lat.at[1], lat_s.at[0], lat_r.at[0], mate)
    for k, f in far:
        i = k * 2 + f
        start(wo_rows(parity, 0, g), wo_rows(parity, k, g), oz_s.at[i], oz_r.at[i], at_pair(k, f))
    spread_o(0, 0)

    local[3].wait()
    step = min(512, width)

    @pl.loop(0, 3 * width // step)
    def _(i):
        cols = pl.ds(pl.multiple_of(i * step, step), step)
        part = jnp.dot(embed_ref[...], wmod[:, cols], preferred_element_type=jnp.float32)
        mod[:, cols] = part[:8]

    def normalize(which):
        block = 16

        @pl.loop(0, tok // block)
        def _(i):
            rows = pl.ds(pl.multiple_of(i * block, block), block)
            values = lat[which, rows, :].astype(jnp.float32)
            center = jnp.mean(values, axis=-1, keepdims=True)
            values = values - center
            spread = jnp.mean(values * values, axis=-1, keepdims=True)
            scaled = values * lax.rsqrt(spread + 1e-06)
            shift = mod[0:1, 0:width]
            scale = mod[0:1, width : 2 * width]
            target = pl.ds(pl.multiple_of(which * tok + i * block, block), block)
            normed[target, :] = (scaled * (1.0 + scale) + shift).astype(jnp.bfloat16)

    def project(k, first, count):
        rows = pl.ds(first, count)
        result = jnp.dot(normed[rows, :], wq[k], preferred_element_type=jnp.float32).astype(jnp.bfloat16)
        q_buf[k, rows, :] = result[:, :head]
        kv[0, k, rows, :] = result[:, head:]

    def share_kv(k, part, first, count):
        rows = pl.ds(first, count)
        for d in range(1, pairs):
            there = (k + d) % pairs
            start(kv.at[0, k, rows, :], kv.at[d, there, rows, :], kv_s.at[d, k, part], kv_r.at[d, there, part], at_pair(d, 0))

    normalize(0)
    pass_q(0)
    for k in range(1, pairs):
        arrive(wq_rows(k, g), wz_s.at[k], wz_r.at[k])
        spread_q(k)
    finish_q(0)
    project(0, 0, tok)
    share_kv(0, 0, 0, tok)
    arrive(lat.at[1], lat_s.at[0], lat_r.at[0])
    normalize(1)
    project(0, tok, tok)
    share_kv(0, 1, tok, tok)
    pass_o(0, 0)
    for k, f in far:
        arrive(wo_rows((parity + f) % 2, k, g), oz_s.at[k * 2 + f], oz_r.at[k * 2 + f])
        spread_o(k, f)
    for k in range(1, pairs):
        pass_q(k)
        finish_q(k)
        project(k, 0, 2 * tok)
        share_kv(k, 0, 0, tok)
        share_kv(k, 1, tok, tok)

    def attend(k):
        for d in range(1, pairs):
            for part in range(2):
                arrive(kv.at[d, k, pl.ds(part * tok, tok), :], kv_s.at[d, k, part], kv_r.at[d, k, part])
        total = pairs * 2 * tok
        keys = kv[:, k, :, :head].reshape(total, head)
        values = kv[:, k, :, head:].reshape(total, head)
        cols = pl.ds(pl.multiple_of((parity * pairs + k) * head, head), head)
        for which in (1, 0):
            query = q_buf[k, pl.ds(which * tok, tok), :]
            scores = lax.dot_general(query, keys, (((1,), (1,)), ((), ())), preferred_element_type=jnp.float32)
            scores = scores / math.sqrt(head)
            largest = jnp.max(scores, axis=1, keepdims=True)
            weights = jnp.exp(scores - largest)
            probs = (weights / jnp.sum(weights, axis=1, keepdims=True)).astype(jnp.bfloat16)
            result = jnp.dot(probs, values, preferred_element_type=jnp.float32).astype(jnp.bfloat16)
            if which == 1:
                att_send[k] = result
                start(att_send.at[k], att_mine.at[:, cols], at_s.at[k], at_r.at[k], mate)
            else:
                att_mine[:, cols] = result

    for k in range(pairs):
        attend(k)
    for k, f in far:
        pass_o(k, f)
    finish_o(0, 0)
    for k, f in far:
        finish_o(k, f)
    for k in range(pairs):
        cols = pl.ds(pl.multiple_of(((1 - parity) * pairs + k) * head, head), head)
        arrive(att_mine.at[:, cols], at_s.at[k], at_r.at[k])

    @pl.loop(0, width // step)
    def _(i):
        cols = pl.ds(pl.multiple_of(i * step, step), step)
        total = jnp.dot(att_mine[...], wo[:, cols], preferred_element_type=jnp.float32)
        gate = mod[0:1, pl.ds(pl.multiple_of(2 * width + i * step, step), step)]
        out_ref[0, :, cols] = (gate * total).astype(jnp.bfloat16)

    for copy in sends:
        copy.wait_send()


def on_device(n_grp, n_sp, latents, timestep, w_mod, w_qkv, w_out):
    _, tok, width = latents.shape
    freq = w_mod.shape[0]
    head = w_qkv.shape[2] // 3
    pairs, chips = n_sp // 2, n_grp // 2
    embed = jnp.broadcast_to(embedding(timestep, freq), (16, freq))
    dma = pltpu.SemaphoreType.DMA
    bf16 = jnp.bfloat16
    anywhere = pl.BlockSpec(memory_space=pl.ANY)
    vmem = pl.BlockSpec(memory_space=pltpu.VMEM)
    return pl.pallas_call(
        functools.partial(kernel, n_grp, n_sp),
        out_shape=jax.ShapeDtypeStruct(latents.shape, bf16),
        in_specs=[anywhere, vmem, anywhere, anywhere, anywhere],
        out_specs=vmem,
        scratch_shapes=[
            pltpu.VMEM((2, tok, width), bf16),
            pltpu.VMEM(w_mod.shape, bf16),
            pltpu.VMEM((8, w_mod.shape[1]), jnp.float32),
            pltpu.VMEM((2 * tok, width), bf16),
            pltpu.VMEM((pairs, width, 3 * head), bf16),
            pltpu.VMEM((n_sp * head, width), bf16),
            pltpu.VMEM((pairs, 2 * tok, head), bf16),
            pltpu.VMEM((pairs, pairs, 2 * tok, 2 * head), bf16),
            pltpu.VMEM((tok, n_sp * head), bf16),
            pltpu.VMEM((pairs, tok, head), bf16),
            dma((4,)),
            dma((pairs,)),
            dma((pairs,)),
            dma((pairs, chips)),
            dma((pairs, chips)),
            dma((pairs, chips)),
            dma((pairs, chips)),
            dma((n_sp,)),
            dma((n_sp,)),
            dma((n_sp, chips)),
            dma((n_sp, chips)),
            dma((n_sp, chips)),
            dma((n_sp, chips)),
            dma((1,)),
            dma((1,)),
            dma((pairs, pairs, 2)),
            dma((pairs, pairs, 2)),
            dma((pairs,)),
            dma((pairs,)),
        ],
        compiler_params=pltpu.CompilerParams(
            collective_id=0, has_side_effects=True, vmem_limit_bytes=64000000
        ),
    )(latents, embed, w_mod, w_qkv, w_out)


def solution(mesh):
    placed = (P("grp", "sp", None), P("grp"), P(), P("sp", "grp", None), P("sp", "grp", None))
    body = functools.partial(on_device, mesh.shape["grp"], mesh.shape["sp"])
    return jax.shard_map(
        body, mesh=mesh, in_specs=placed, out_specs=P("grp", "sp", None), check_vma=False
    )
```

time: 185 us -> 60.3 us (0.33)
  waiting for transfers between devices: 126 us -> 0 us
  Pallas kernels: 0 us -> 55.9 us
  blocking collectives: 25.8 us -> 0 us
  between operations: 13.9 us -> 0.67 us
  matrix products: 11.1 us -> 0 us
  other arithmetic: 7.36 us -> 0.06 us
    all_gather x3 -> x0, waiting for transfers between devices: 125 us -> none  [the longest x1 65 us: on_device(): whole = lax.all_gather(normed, 'sp', axis=1, tiled=True)]
    pallas_call x0 -> x1, Pallas kernels: none -> 55.9 us  [on_device(): pl.pallas_call(functools.partial(kernel, n_grp, n_sp), out_shape=jax.Shap...]
    all_gather x1 -> x0, blocking collectives: 14.1 us -> none  [on_device(): out_rows = lax.all_gather(w_out, 'grp', axis=1, tiled=True)]
    all_to_all x1 -> x0, blocking collectives: 11.8 us -> none  [on_device(): lax.all_to_all(attended, 'sp', split_axis=1, concat_axis=2, tiled=True)]
    dot_general x5 -> x0, matrix products: 11.1 us -> none  [the longest x1 4.41 us: on_device(): jnp.einsum('itc,cf->itf', whole, lax.all_gather(w_qkv, 'grp', axis=1, til...]
    reduce_sum x4 -> x0, other arithmetic: 3.56 us -> none  [the longest x1 1.49 us: normalize(): spread = jnp.mean((values - center) ** 2, axis=-1, keepdims=True)]
    convert_element_type x2 -> x0, other arithmetic: 2.27 us -> none  [the longest x1 1.27 us: normalize(): (normed * (1.0 + scale[:, None, :]) + shift[:, None, :]).astype(jnp.bfloa...]
  transfers between devices with their start and end apart: 3 -> 0, of which waited for: 3 -> 0; matrix products, arithmetic and copies ran while one was open for 8% -> 0% of each run, Pallas kernels for 0% -> 0%
where the time goes in v1:
time: 60.3 us; the launch traced here: 59.3 us
  Pallas kernels  55.9 us (93%)
  local copies, waits for them, and re-layouts  2.67 us (4%)
  between operations  0.67 us (1%)
    pallas_call x1, Pallas kernels, on_device(): pl.pallas_call(functools.partial(kernel, n_grp, n_sp), out_shape=jax.Shap...  55.9 us
    unnamed x1, local copies, waits for them, and re-layouts  2.06 us

profile of v1, /device:TPU:0, one launch (start us, length us, event | category | flops | bytes accessed | tf_op | source)
XLA Modules:
  0.0 59.3 jit_solution(5129884829412473766)
XLA Ops:
  0.7 0.1 sine_convert_fusion
  0.7 0.6 %broadcast_in_dim.2.embed_ref = bf16[16,256]{1,0:T(8,128)(2,1)} broadcast(bf16[256]{0:T(256)(128)(2,1)S(1)} %pad_maximum_fusion), dimensions={1} | broadcast | bytes 8704 | tf_op jit(solution)/shard_map/broadcast_in_dim | solution.py:276
  1.3 55.9 %shard_map.55 = bf16[1,128,3072]{2,1,0:T(8,128)(2,1)} custom-call(bf16[1,128,3072]{2,1,0:T(8,128)(2,1)} %lat_hbm.1, bf16[16,256]{1,0:T(8,128)(2,1)} %broadcast_in_dim.2.embed_ref, bf16[256,9216]{1,0:T(8,128)(2,1)} %wmod_hbm.1, bf16[1,384,384]{2,1,0:T(8,128)(2,1)} %wqkv_hbm.1, bf16[1,16,3072]{2,1,0:T(8,128)(2,1)} %wout_hbm.1), custom_call_target="tpu_custom_call" | custom-call | tf_op jit(solution)/shard_map/pallas_call | solution.py:281
  57.2 2.1 %copy.8 = bf16[1,128,3072]{2,1,0:T(8,128)(2,1)} copy(bf16[1,128,3072]{2,1,0:T(8,128)(2,1)} %shard_map.55) | data formatting | bytes 1572864
  (1 shorter events, 0.0 us)

commit v2 on v1

--- a/solution.py
+++ b/solution.py
@@ -9,6 +9,7 @@
 from jax.sharding import PartitionSpec as P
 
 MESH = pl.DeviceIdType.MESH
+CHUNKS = 4
 
 
 def embedding(timestep, freq):
@@ -116,53 +117,99 @@
     def arrive(region, ssem, rsem):
         remote(region, region, ssem, rsem, sib).wait_recv()
 
+    square = chips == 4
+    near_x = chip // 2 * 2 + 1 - chip % 2
+    near_y = (chip + 2) % 4
+    corner = (near_x + 2) % 4
+    to_x, to_y = (near_x * 2 + core, s), (near_y * 2 + core, s)
+    others = [near_x, near_y, corner] if square else [(chip + chips - c) % chips for c in range(1, chips)]
+
+    def q_part(k, owner, half):
+        size = rows_q // 2
+        return wq.at[k, pl.ds(pl.multiple_of(owner * rows_q + half * size, size), size), :]
+
+    def o_part(par, k, owner, half):
+        first = (par * pairs + k) * head + owner * rows_o
+        size = width // 2
+        return wo.at[pl.ds(pl.multiple_of(first, rows_o), rows_o), half * size : (half + 1) * size]
+
+    class Spread:
+        def __init__(self, i, whole, part, xs, xr, ds, dr):
+            self.i, self.whole, self.part = i, whole, part
+            self.xs, self.xr, self.ds, self.dr = xs, xr, ds, dr
+
+        def cross(self, region, slot, device):
+            start(region, region, self.xs.at[self.i, slot], self.xr.at[self.i, slot], device)
+
+        def land(self, region, slot):
+            arrive(region, self.xs.at[self.i, slot], self.xr.at[self.i, slot])
+
+        def to_sib(self, region, slot):
+            start(region, region, self.ds.at[self.i, slot], self.dr.at[self.i, slot], sib)
+
+        def begin(self):
+            mine = self.whole(g)
+            if square:
+                self.cross(mine, 0, to_x)
+                self.cross(mine, 1, to_y)
+            else:
+                for c in range(1, chips):
+                    self.cross(mine, c - 1, at_chip(c))
+            self.to_sib(mine, 0)
+
+        def relay(self):
+            if square:
+                for slot, device in ((0, to_y), (1, to_x)):
+                    owner = others[slot] * 2 + core
+                    self.land(self.whole(owner), slot)
+                    self.cross(self.part(owner, slot), 2 + slot, device)
+                    self.to_sib(self.whole(owner), 1 + slot)
+            else:
+                for slot in range(chips - 1):
+                    region = self.whole(others[slot] * 2 + core)
+                    self.land(region, slot)
+                    self.to_sib(region, 1 + slot)
+
+        def last(self):
+            if square:
+                owner = corner * 2 + core
+                self.land(self.part(owner, 0), 2)
+                self.land(self.part(owner, 1), 3)
+                self.to_sib(self.whole(owner), 3)
+
+        def finish(self):
+            for slot, owner in enumerate([chip] + others):
+                arrive(self.whole(owner * 2 + 1 - core), self.ds.at[self.i, slot], self.dr.at[self.i, slot])
+
+    def spread_q(k):
+        return Spread(k, functools.partial(wq_rows, k), functools.partial(q_part, k), wx_s, wx_r, wd_s, wd_r)
+
+    def spread_o(k, flip):
+        par = (parity + flip) % 2
+        whole, part = functools.partial(wo_rows, par, k), functools.partial(o_part, par, k)
+        return Spread(k * 2 + flip, whole, part, ox_s, ox_r, od_s, od_r)
+
+    far = [(k, f) for k in range(pairs) for f in range(2) if (k, f) != (0, 0)]
+    all_q = [spread_q(k) for k in range(pairs)]
+    near_o, far_o = spread_o(0, 0), [spread_o(k, f) for k, f in far]
+
+    def land_o(n):
+        k, f = far[n]
+        i = k * 2 + f
+        arrive(wo_rows((parity + f) % 2, k, g), oz_s.at[i], oz_r.at[i])
+        far_o[n].begin()
+
+    all_q[0].begin()
     for k in range(1, pairs):
         start(wq_rows(0, g), wq_rows(k, g), wz_s.at[k], wz_r.at[k], at_pair(k, 0))
-
-    def spread_q(k):
-        for c in range(1, chips):
-            start(wq_rows(k, g), wq_rows(k, g), wx_s.at[k, c], wx_r.at[k, c], at_chip(c))
-        start(wq_rows(k, g), wq_rows(k, g), wd_s.at[k, 0], wd_r.at[k, 0], sib)
-
-    def pass_q(k):
-        for c in range(1, chips):
-            region = wq_rows(k, (chip + chips - c) % chips * 2 + core)
-            arrive(region, wx_s.at[k, c], wx_r.at[k, c])
-            start(region, region, wd_s.at[k, c], wd_r.at[k, c], sib)
-
-    def finish_q(k):
-        for c in range(chips):
-            region = wq_rows(k, (chip + chips - c) % chips * 2 + 1 - core)
-            arrive(region, wd_s.at[k, c], wd_r.at[k, c])
-
-    def spread_o(k, flip):
-        region = wo_rows((parity + flip) % 2, k, g)
-        i = k * 2 + flip
-        for c in range(1, chips):
-            start(region, region, ox_s.at[i, c], ox_r.at[i, c], at_chip(c))
-        start(region, region, od_s.at[i, 0], od_r.at[i, 0], sib)
-
-    def pass_o(k, flip):
-        i = k * 2 + flip
-        for c in range(1, chips):
-            region = wo_rows((parity + flip) % 2, k, (chip + chips - c) % chips * 2 + core)
-            arrive(region, ox_s.at[i, c], ox_r.at[i, c])
-            start(region, region, od_s.at[i, c], od_r.at[i, c], sib)
-
-    def finish_o(k, flip):
-        i = k * 2 + flip
-        for c in range(chips):
-            region = wo_rows((parity + flip) % 2, k, (chip + chips - c) % chips * 2 + 1 - core)
-            arrive(region, od_s.at[i, c], od_r.at[i, c])
-
-    far = [(k, f) for k in range(pairs) for f in range(2) if (k, f) != (0, 0)]
-
-    spread_q(0)
-    start(lat.at[0], lat.at[1], lat_s.at[0], lat_r.at[0], mate)
     for k, f in far:
         i = k * 2 + f
         start(wo_rows(parity, 0, g), wo_rows(parity, k, g), oz_s.at[i], oz_r.at[i], at_pair(k, f))
-    spread_o(0, 0)
+    piece = tok // CHUNKS
+    for c in range(CHUNKS):
+        rows = pl.ds(c * piece, piece)
+        start(lat.at[0, rows, :], lat.at[1, rows, :], lat_s.at[c], lat_r.at[c], mate)
+    near_o.begin()
 
     local[3].wait()
     step = min(512, width)
@@ -173,12 +220,12 @@
         part = jnp.dot(embed_ref[...], wmod[:, cols], preferred_element_type=jnp.float32)
         mod[:, cols] = part[:8]
 
-    def normalize(which):
+    def normalize(which, first, count):
         block = 16
 
-        @pl.loop(0, tok // block)
+        @pl.loop(0, count // block)
         def _(i):
-            rows = pl.ds(pl.multiple_of(i * block, block), block)
+            rows = pl.ds(pl.multiple_of(first + i * block, block), block)
             values = lat[which, rows, :].astype(jnp.float32)
             center = jnp.mean(values, axis=-1, keepdims=True)
             values = values - center
@@ -186,48 +233,69 @@
             scaled = values * lax.rsqrt(spread + 1e-06)
             shift = mod[0:1, 0:width]
             scale = mod[0:1, width : 2 * width]
-            target = pl.ds(pl.multiple_of(which * tok + i * block, block), block)
+            target = pl.ds(pl.multiple_of(which * tok + first + i * block, block), block)
             normed[target, :] = (scaled * (1.0 + scale) + shift).astype(jnp.bfloat16)
 
-    def project(k, first, count):
-        rows = pl.ds(first, count)
+    def normalize_chunk(c):
+        region = lat.at[1, pl.ds(c * piece, piece), :]
+        arrive(region, lat_s.at[c], lat_r.at[c])
+        normalize(1, c * piece, piece)
+
+    spans = [(0, tok), (tok, tok - piece), (2 * tok - piece, piece)]
+
+    def project(k, part):
+        rows = pl.ds(*spans[part])
         result = jnp.dot(normed[rows, :], wq[k], preferred_element_type=jnp.float32).astype(jnp.bfloat16)
         q_buf[k, rows, :] = result[:, :head]
         kv[0, k, rows, :] = result[:, head:]
 
-    def share_kv(k, part, first, count):
-        rows = pl.ds(first, count)
+    def share_kv(k, part):
+        rows = pl.ds(*spans[part])
         for d in range(1, pairs):
             there = (k + d) % pairs
             start(kv.at[0, k, rows, :], kv.at[d, there, rows, :], kv_s.at[d, k, part], kv_r.at[d, there, part], at_pair(d, 0))
 
-    normalize(0)
-    pass_q(0)
+    normalize(0, 0, tok)
+    all_q[0].relay()
+    near_o.relay()
     for k in range(1, pairs):
         arrive(wq_rows(k, g), wz_s.at[k], wz_r.at[k])
-        spread_q(k)
-    finish_q(0)
-    project(0, 0, tok)
-    share_kv(0, 0, 0, tok)
-    arrive(lat.at[1], lat_s.at[0], lat_r.at[0])
-    normalize(1)
-    project(0, tok, tok)
-    share_kv(0, 1, tok, tok)
-    pass_o(0, 0)
-    for k, f in far:
-        arrive(wo_rows((parity + f) % 2, k, g), oz_s.at[k * 2 + f], oz_r.at[k * 2 + f])
-        spread_o(k, f)
+        all_q[k].begin()
+    land_o(0)
+    all_q[0].last()
+    near_o.last()
+    all_q[0].finish()
+    project(0, 0)
+    share_kv(0, 0)
     for k in range(1, pairs):
-        pass_q(k)
-        finish_q(k)
-        project(k, 0, 2 * tok)
-        share_kv(k, 0, 0, tok)
-        share_kv(k, 1, tok, tok)
+        all_q[k].relay()
+    for n in range(1, len(far)):
+        land_o(n)
+    normalize_chunk(0)
+    far_o[0].relay()
+    for k in range(1, pairs):
+        all_q[k].last()
+        all_q[k].finish()
+        project(k, 0)
+        share_kv(k, 0)
+    for c in range(1, CHUNKS - 1):
+        normalize_chunk(c)
+    for k in range(pairs):
+        project(k, 1)
+        share_kv(k, 1)
+    for n in range(1, len(far)):
+        far_o[n].relay()
+    normalize_chunk(CHUNKS - 1)
+    for k in range(pairs):
+        project(k, 2)
+        share_kv(k, 2)
+    for spread in far_o:
+        spread.last()
 
     def attend(k):
         for d in range(1, pairs):
-            for part in range(2):
-                arrive(kv.at[d, k, pl.ds(part * tok, tok), :], kv_s.at[d, k, part], kv_r.at[d, k, part])
+            for part, span in enumerate(spans):
+                arrive(kv.at[d, k, pl.ds(*span), :], kv_s.at[d, k, part], kv_r.at[d, k, part])
         total = pairs * 2 * tok
         keys = kv[:, k, :, :head].reshape(total, head)
         values = kv[:, k, :, head:].reshape(total, head)
@@ -248,11 +316,8 @@
 
     for k in range(pairs):
         attend(k)
-    for k, f in far:
-        pass_o(k, f)
-    finish_o(0, 0)
-    for k, f in far:
-        finish_o(k, f)
+    for spread in [near_o] + far_o:
+        spread.finish()
     for k in range(pairs):
         cols = pl.ds(pl.multiple_of(((1 - parity) * pairs + k) * head, head), head)
         arrive(att_mine.at[:, cols], at_s.at[k], at_r.at[k])
@@ -307,10 +372,10 @@
             dma((n_sp, chips)),
             dma((n_sp, chips)),
             dma((n_sp, chips)),
-            dma((1,)),
-            dma((1,)),
-            dma((pairs, pairs, 2)),
-            dma((pairs, pairs, 2)),
+            dma((CHUNKS,)),
+            dma((CHUNKS,)),
+            dma((pairs, pairs, 3)),
+            dma((pairs, pairs, 3)),
             dma((pairs,)),
             dma((pairs,)),
         ],

time: 60.3 us -> 59.4 us (0.985); the launches traced: 59.3 us -> 59.2 us
  no operation moved by 1% of the time
where the time goes in v2:
time: 59.4 us; the launch traced here: 59.2 us
  Pallas kernels  55.8 us (94%)
  local copies, waits for them, and re-layouts  2.67 us (4%)
  between operations  0.67 us (1%)
    pallas_call x1, Pallas kernels, on_device(): pl.pallas_call(functools.partial(kernel, n_grp, n_sp), out_shape=jax.Shap...  55.8 us
    unnamed x1, local copies, waits for them, and re-layouts  2.06 us

profile of v2, /device:TPU:0, one launch (start us, length us, event | category | flops | bytes accessed | tf_op | source)
XLA Modules:
  0.0 59.2 jit_solution(1156735009630564928)
XLA Ops:
  0.7 0.1 sine_convert_fusion
  0.7 0.6 %broadcast_in_dim.2.embed_ref = bf16[16,256]{1,0:T(8,128)(2,1)} broadcast(bf16[256]{0:T(256)(128)(2,1)S(1)} %pad_maximum_fusion), dimensions={1} | broadcast | bytes 8704 | tf_op jit(solution)/shard_map/broadcast_in_dim | solution.py:341
  1.3 55.8 %shard_map.55 = bf16[1,128,3072]{2,1,0:T(8,128)(2,1)} custom-call(bf16[1,128,3072]{2,1,0:T(8,128)(2,1)} %lat_hbm.1, bf16[16,256]{1,0:T(8,128)(2,1)} %broadcast_in_dim.2.embed_ref, bf16[256,9216]{1,0:T(8,128)(2,1)} %wmod_hbm.1, bf16[1,384,384]{2,1,0:T(8,128)(2,1)} %wqkv_hbm.1, bf16[1,16,3072]{2,1,0:T(8,128)(2,1)} %wout_hbm.1), custom_call_target="tpu_custom_call" | custom-call | tf_op jit(solution)/shard_map/pallas_call | solution.py:346
  57.1 2.1 %copy.8 = bf16[1,128,3072]{2,1,0:T(8,128)(2,1)} copy(bf16[1,128,3072]{2,1,0:T(8,128)(2,1)} %shard_map.55) | data formatting | bytes 1572864
  (1 shorter events, 0.0 us)

commit v3 on v2

--- a/solution.py
+++ b/solution.py
@@ -16,18 +16,19 @@
     half_freq = freq // 2
     freqs = jnp.exp(-math.log(10000.0) * jnp.arange(half_freq, dtype=jnp.float32) / half_freq)
     angles = timestep.astype(jnp.float32)[:, None] * freqs[None, :]
-    return jnp.concatenate([jnp.cos(angles), jnp.sin(angles)], axis=1).astype(jnp.bfloat16)
+    return jnp.cos(angles), jnp.sin(angles)
 
 
 def kernel(
     n_grp,
     n_sp,
     lat_hbm,
-    embed_ref,
+    cos_ref,
+    sin_ref,
     wmod_hbm,
     wqkv_hbm,
     wout_hbm,
-    out_ref,
+    out_hbm,
     lat,
     wmod,
     mod,
@@ -38,6 +39,7 @@
     kv,
     att_mine,
     att_send,
+    out_buf,
     loc_sem,
     wz_s,
     wz_r,
@@ -202,22 +204,29 @@
     all_q[0].begin()
     for k in range(1, pairs):
         start(wq_rows(0, g), wq_rows(k, g), wz_s.at[k], wz_r.at[k], at_pair(k, 0))
-    for k, f in far:
-        i = k * 2 + f
-        start(wo_rows(parity, 0, g), wo_rows(parity, k, g), oz_s.at[i], oz_r.at[i], at_pair(k, f))
+
+    def send_o(n):
+        for k, f in far[n : n + 1]:
+            i = k * 2 + f
+            start(wo_rows(parity, 0, g), wo_rows(parity, k, g), oz_s.at[i], oz_r.at[i], at_pair(k, f))
+
     piece = tok // CHUNKS
-    for c in range(CHUNKS):
+
+    def send_chunk(c):
         rows = pl.ds(c * piece, piece)
         start(lat.at[0, rows, :], lat.at[1, rows, :], lat_s.at[c], lat_r.at[c], mate)
-    near_o.begin()
+
+    send_chunk(0)
 
     local[3].wait()
     step = min(512, width)
+    embed = jnp.concatenate([cos_ref[...], sin_ref[...]], axis=1).astype(jnp.bfloat16)
+    embed = jnp.broadcast_to(embed, (16, embed.shape[1]))
 
     @pl.loop(0, 3 * width // step)
     def _(i):
         cols = pl.ds(pl.multiple_of(i * step, step), step)
-        part = jnp.dot(embed_ref[...], wmod[:, cols], preferred_element_type=jnp.float32)
+        part = jnp.dot(embed, wmod[:, cols], preferred_element_type=jnp.float32)
         mod[:, cols] = part[:8]
 
     def normalize(which, first, count):
@@ -257,40 +266,47 @@
 
     normalize(0, 0, tok)
     all_q[0].relay()
-    near_o.relay()
+    near_o.begin()
+    send_chunk(1)
     for k in range(1, pairs):
         arrive(wq_rows(k, g), wz_s.at[k], wz_r.at[k])
         all_q[k].begin()
-    land_o(0)
+    send_o(0)
+    send_chunk(2)
+    send_o(1)
+    send_chunk(3)
+    for n in range(2, len(far)):
+        send_o(n)
     all_q[0].last()
-    near_o.last()
+    near_o.relay()
     all_q[0].finish()
     project(0, 0)
     share_kv(0, 0)
+    near_o.last()
     for k in range(1, pairs):
         all_q[k].relay()
-    for n in range(1, len(far)):
-        land_o(n)
     normalize_chunk(0)
-    far_o[0].relay()
     for k in range(1, pairs):
         all_q[k].last()
         all_q[k].finish()
         project(k, 0)
         share_kv(k, 0)
+    land_o(0)
+    land_o(1)
     for c in range(1, CHUNKS - 1):
         normalize_chunk(c)
     for k in range(pairs):
         project(k, 1)
         share_kv(k, 1)
-    for n in range(1, len(far)):
-        far_o[n].relay()
     normalize_chunk(CHUNKS - 1)
     for k in range(pairs):
         project(k, 2)
         share_kv(k, 2)
-    for spread in far_o:
-        spread.last()
+    far_o[0].relay()
+    for n in range(2, len(far)):
+        land_o(n)
+    far_o[1].relay()
+    far_o[0].last()
 
     def attend(k):
         for d in range(1, pairs):
@@ -314,21 +330,29 @@
             else:
                 att_mine[:, cols] = result
 
-    for k in range(pairs):
+    attend(0)
+    for spread in far_o[2:]:
+        spread.relay()
+    far_o[1].last()
+    for k in range(1, pairs):
         attend(k)
+    for spread in far_o[2:]:
+        spread.last()
     for spread in [near_o] + far_o:
         spread.finish()
     for k in range(pairs):
         cols = pl.ds(pl.multiple_of(((1 - parity) * pairs + k) * head, head), head)
         arrive(att_mine.at[:, cols], at_s.at[k], at_r.at[k])
-
-    @pl.loop(0, width // step)
-    def _(i):
-        cols = pl.ds(pl.multiple_of(i * step, step), step)
+    outs = []
+    for i in range(width // step):
+        cols = slice(i * step, (i + 1) * step)
         total = jnp.dot(att_mine[...], wo[:, cols], preferred_element_type=jnp.float32)
-        gate = mod[0:1, pl.ds(pl.multiple_of(2 * width + i * step, step), step)]
-        out_ref[0, :, cols] = (gate * total).astype(jnp.bfloat16)
-
+        gate = mod[0:1, 2 * width + i * step : 2 * width + (i + 1) * step]
+        out_buf[:, cols] = (gate * total).astype(jnp.bfloat16)
+        outs.append(pltpu.make_async_copy(out_buf.at[:, cols], out_hbm.at[0, :, cols], loc_sem.at[4 + i]))
+        outs[i].start()
+    for copy in outs:
+        copy.wait()
     for copy in sends:
         copy.wait_send()
 
@@ -338,7 +362,7 @@
     freq = w_mod.shape[0]
     head = w_qkv.shape[2] // 3
     pairs, chips = n_sp // 2, n_grp // 2
-    embed = jnp.broadcast_to(embedding(timestep, freq), (16, freq))
+    cos, sin = embedding(timestep, freq)
     dma = pltpu.SemaphoreType.DMA
     bf16 = jnp.bfloat16
     anywhere = pl.BlockSpec(memory_space=pl.ANY)
@@ -346,8 +370,8 @@
     return pl.pallas_call(
         functools.partial(kernel, n_grp, n_sp),
         out_shape=jax.ShapeDtypeStruct(latents.shape, bf16),
-        in_specs=[anywhere, vmem, anywhere, anywhere, anywhere],
-        out_specs=vmem,
+        in_specs=[anywhere, vmem, vmem, anywhere, anywhere, anywhere],
+        out_specs=anywhere,
         scratch_shapes=[
             pltpu.VMEM((2, tok, width), bf16),
             pltpu.VMEM(w_mod.shape, bf16),
@@ -359,7 +383,8 @@
             pltpu.VMEM((pairs, pairs, 2 * tok, 2 * head), bf16),
             pltpu.VMEM((tok, n_sp * head), bf16),
             pltpu.VMEM((pairs, tok, head), bf16),
-            dma((4,)),
+            pltpu.VMEM((tok, width), bf16),
+            dma((4 + width // min(512, width),)),
             dma((pairs,)),
             dma((pairs,)),
             dma((pairs, chips)),
@@ -382,7 +407,7 @@
         compiler_params=pltpu.CompilerParams(
             collective_id=0, has_side_effects=True, vmem_limit_bytes=64000000
         ),
-    )(latents, embed, w_mod, w_qkv, w_out)
+    )(latents, cos, sin, w_mod, w_qkv, w_out)
 
 
 def solution(mesh):

time: 59.4 us -> 58.2 us (0.980); the launches traced: 59.2 us -> 57.2 us
  Pallas kernels: 55.8 us -> 53.9 us
  local copies, waits for them, and re-layouts: 2.67 us -> 2.06 us
    pallas_call x1, Pallas kernels: 55.8 us -> 53.9 us  [on_device(): pl.pallas_call(functools.partial(kernel, n_grp, n_sp), out_shape=jax.Shap...]
    broadcast_in_dim x1 -> x0, local copies, waits for them, and re-layouts: 0.61 us -> none  [on_device(): embed = jnp.broadcast_to(embedding(timestep, freq), (16, freq))]
    sin x0 -> x1, other arithmetic: none -> 0.6 us  [embedding(): return (jnp.cos(angles), jnp.sin(angles))]
where the time goes in v3:
time: 58.2 us; the launch traced here: 57.2 us
  Pallas kernels  53.9 us (93%)
  local copies, waits for them, and re-layouts  2.06 us (4%)
  between operations  0.66 us (1%)
  other arithmetic  0.6 us (1%)
    pallas_call x1, Pallas kernels, on_device(): pl.pallas_call(functools.partial(kernel, n_grp, n_sp), out_shape=jax.Shap...  53.9 us
    unnamed x1, local copies, waits for them, and re-layouts  2.06 us

profile of v3, /device:TPU:0, one launch (start us, length us, event | category | flops | bytes accessed | tf_op | source)
XLA Modules:
  0.0 57.2 jit_solution(4594385823026354209)
XLA Ops:
  0.7 0.6 %fusion = (f32[1,128]{1,0:T(1,128)}, f32[1,128]{1,0:T(1,128)}) fusion(f32[]{:T(128)} %bitcast), kind=kLoop, calls=%fused_computation.1 | loop fusion | flops 256 | bytes 1028 | tf_op jit(solution)/shard_map/sin | solution.py:19
  1.3 53.9 %shard_map.55 = bf16[1,128,3072]{2,1,0:T(8,128)(2,1)} custom-call(bf16[1,128,3072]{2,1,0:T(8,128)(2,1)} %lat_hbm.1, f32[1,128]{1,0:T(1,128)} %get-tuple-element.6.cos_ref, f32[1,128]{1,0:T(1,128)} %get-tuple-element.5.sin_ref, bf16[256,9216]{1,0:T(8,128)(2,1)} %wmod_hbm.1, bf16[1,384,384]{2,1,0:T(8,128)(2,1)} %wqkv_hbm.1, bf16[1,16,3072]{2,1,0:T(8,128)(2,1)} %wout_hbm.1), custom_call_target="tpu_custom_call" | custom-call | tf_op jit(solution)/shard_map/pallas_call | solution.py:370
  55.2 2.1 %copy.8 = bf16[1,128,3072]{2,1,0:T(8,128)(2,1)} copy(bf16[1,128,3072]{2,1,0:T(8,128)(2,1)} %shard_map.55) | data formatting | bytes 1572864
